TPU v7x, 32 devices: a whole 2x2x4 slice. The times are simulated.
32 devices in a mesh: groups: 2 (over y), ep: 4 (over x, core), tp: 4 (over z).
Axes of the slice: x: 2, y: 2, z: 4, core: 2. Of those that a mesh axis runs over, the one named last changes fastest.
Arguments:
- tokens: bfloat16 [256, 7168], P(('groups', 'ep')), parts along dimension 0, may hold values from -6 to 6
- w_gate: bfloat16 [16, 7168, 2048], P('ep', None, 'tp'), may hold values from -0.0625 to 0.0625
- w_up: bfloat16 [16, 7168, 2048], P('ep', None, 'tp'), may hold values from -0.0625 to 0.0625
- w_down: bfloat16 [16, 2048, 7168], P('ep', 'tp'), may hold values from -0.1875 to 0.1875
- router_logits: float32 [256, 8], P(('groups', 'ep')), parts along dimension 0, may hold values from -6 to 6
- expert_ids: int32 [256, 8], P(('groups', 'ep')), parts along dimension 0, may hold values from 0 to 15, all different within a row; in each aligned block of 32 rows (0 to 31, 32 to 63, ...) at most 24 rows name the same one
- draft_lengths: int32 [32], P(('groups', 'ep')), parts along dimension 0, may hold values from 7 to 8
- accept_mask: int32 [32, 8], P(('groups', 'ep')), parts along dimension 0, may hold values 0 or 1
Outputs:
- mixed: bfloat16 [256, 7168], P(('groups', 'ep'), 'tp'), parts along dimension 0
- accepted: int32 [2], P('groups'), parts along dimension 0
There are 2 independent parts, one for each index of `groups`. A program takes and returns all parts, laid end to end along the dimension named above; an argument that names none is the same for every part. Nothing has to cross between parts.
Inputs may be any that keep to these rules, and one draw needn't show every extreme that they name: `expert_ids`: each row names 8 different experts. Among the rows of one ep index (aligned blocks of 32 rows) no expert is named by more than 24 rows, and in every draw some expert is named by exactly 24 rows of some block.
All inputs are finite; a program needn't handle non-finite values. No bound on the sum of `accept_mask` on one device may be relied on, other than what follows from the above.
Results may differ from a plain program's by a relative error of at most 0.017.
Values may be sent and summed in bfloat16 or wider, within the bound.
A program may use at most 192 MiB of HBM per device.

v0:
```python
import jax
import jax.numpy as jnp
from jax import lax
from jax.sharding import PartitionSpec as P

DRAFT = 8
EXPERTS = 16


def per_device(tokens, w_gate, w_up, w_down, router_logits, expert_ids, draft_lengths, accept_mask):
    tok_rows = tokens.shape[0]
    local = w_gate.shape[0]
    me = lax.axis_index("ep")
    live = jnp.arange(DRAFT, dtype=jnp.int32)[None, :] < draft_lengths[:, None]
    sig = jax.nn.sigmoid(router_logits)
    gates = 2.827 * sig / jnp.sum(sig, axis=1, keepdims=True)
    named = expert_ids[:, :, None] == jnp.arange(EXPERTS, dtype=jnp.int32)[None, None, :]
    dense = jnp.sum(jnp.where(named, gates[:, :, None], 0.0), axis=1)
    dense = jnp.where(live.reshape(tok_rows)[:, None], dense, 0.0)
    rows = lax.all_gather(tokens, "ep", axis=0, tiled=True)
    dense = lax.all_gather(dense, "ep", axis=0, tiled=True)
    mine = lax.dynamic_slice_in_dim(dense, me * local, local, axis=1)
    gate = jnp.einsum("md,edf->emf", rows, w_gate, preferred_element_type=jnp.float32)
    up = jnp.einsum("md,edf->emf", rows, w_up, preferred_element_type=jnp.float32)
    hidden = (jax.nn.silu(gate) * up * mine.T[:, :, None]).astype(jnp.bfloat16)
    partial = jnp.einsum("emf,efd->md", hidden, w_down, preferred_element_type=jnp.float32)
    partial = partial.astype(jnp.bfloat16)
    partial = lax.psum_scatter(partial, "ep", scatter_dimension=0, tiled=True)
    mixed = lax.psum_scatter(partial, "tp", scatter_dimension=1, tiled=True)
    passed = accept_mask * live.astype(jnp.int32)
    accepted = lax.psum(jnp.sum(jnp.cumprod(passed, axis=1)), "ep").reshape(1)
    return (mixed, accepted)


def solution(mesh):
    placed = (
        P(("groups", "ep"), None),
        P("ep", None, "tp"),
        P("ep", None, "tp"),
        P("ep", "tp", None),
        P(("groups", "ep"), None),
        P(("groups", "ep"), None),
        P(("groups", "ep")),
        P(("groups", "ep"), None),
    )
    return jax.shard_map(
        per_device,
        mesh=mesh,
        in_specs=placed,
        out_specs=(P(("groups", "ep"), "tp"), P("groups")),
        check_vma=False,
    )
```

profile of v0, /device:TPU:0, one launch (start us, length us, event | category | flops | bytes accessed | tf_op | source)
XLA Modules:
  0.0 140.5 jit_solution(3762252298330406964)
XLA Ops:
  7.2 0.0 all-gather.3.cloned.1.call-start
  7.2 0.7 all-gather.3.cloned.1.call-update
  7.9 0.0 reduce-scatter.3.cloned.1.call-start
  7.9 0.7 iota_compare_fusion.1
  8.7 0.1 lt.26
  8.8 0.7 fusion.20
  9.5 0.7 multiply_divide_fusion
  10.2 0.7 select_reduce_fusion
  10.9 6.2 %all-gather = f32[4,32,16]{1,2,0:T(8,128)S(1)} all-gather(f32[1,32,16]{1,2,0:T(8,128)S(1)} %select_bitcast_fusion), channel_id=1, replica_groups=mesh['groups'=2,'ep'=4,'tp'=4] {'ep'}, dimensions={0}, use_global_device_ids=true | all-gather | bytes 10240 | tf_op jit(solution)/shard_map/all_gather | solution.py:21
  17.1 0.1 reshape.28
  17.2 16.2 %all-gather.3.cloned.1.call-done = bf16[128,7168]{1,0:T(8,128)(2,1)} async-done(((bf16[32,7168]{1,0:T(8,128)(2,1)}), bf16[128,7168]{1,0:T(8,128)(2,1)}) %all-gather.3.cloned.1.call-update) | async-done | bytes 1835024 | tf_op jit(solution)/shard_map/all_gather | solution.py:20
  33.4 17.8 %fusion.5 = f32[4,128,512]{1,2,0:T(8,128)S(1)} fusion(bf16[4,7168,512]{2,1,0:T(8,128)(2,1)} %param.9, bf16[128,7168]{1,0:T(8,128)(2,1)} %all-gather.3.cloned.1.call-done), kind=kOutput, calls=%fused_computation.6 | convolution fusion | flops 3758096384 | bytes 32243712 | tf_op jit(solution)/shard_map/md,edf->emf/dot_general | solution.py:23
  51.2 0.0 copy-start.1
  51.2 14.0 %fusion.17 = bf16[4,128,512]{1,2,0:T(8,128)(2,1)S(1)} fusion(bf16[4,7168,512]{2,1,0:T(8,128)(2,1)} %param.10, bf16[128,7168]{1,0:T(8,128)(2,1)S(1)} %copy-done.2, f32[4,128,512]{1,2,0:T(8,128)S(1)} %fusion.5, f32[4,128]{1,0:T(4,128)S(1)} %dynamic-slice_bitcast_fusion), kind=kOutput, calls=%fused_computation.10 | convolution fusion | flops 3759931392 | bytes 32770048 | tf_op jit(solution)/shard_map/md,edf->emf/dot_general | solution.py:24
  65.2 14.8 %fusion = bf16[128,7168]{1,0:T(8,128)(2,1)} fusion(bf16[4,128,512]{1,2,0:T(8,128)(2,1)S(1)} %fusion.17, bf16[4,512,7168]{2,1,0:T(8,128)(2,1)} %param.11), kind=kOutput, calls=%fused_computation.1 | convolution fusion | flops 3759013888 | bytes 31719424 | tf_op jit(solution)/shard_map/emf,efd->md/dot_general | solution.py:26
  80.0 0.0 reduce-scatter.3.cloned.1.call-update
  80.0 0.0 reduce-scatter.5.cloned.1.call-start
  80.1 29.7 %reduce-scatter.3.cloned.1.call-done = bf16[32,7168]{1,0:T(8,128)(2,1)} async-done(((bf16[128,7168]{1,0:T(8,128)(2,1)}), bf16[32,7168]{1,0:T(8,128)(2,1)}) %reduce-scatter.3.cloned.1.call-update) | async-done | bytes 458768 | tf_op jit(solution)/shard_map/reduce_scatter | solution.py:28
  109.8 0.0 reduce-scatter.5.cloned.1.call-update
  109.8 0.1 broadcast_select_fusion
  109.9 0.2 reduce_window.9
  110.1 0.6 reduce_sum.29
  110.7 4.9 %psum.7 = s32[1]{0:T(128)} all-reduce(s32[1]{0:T(128)} %bitcast.6), channel_id=1, replica_groups=mesh['groups'=2,'ep'=4,'tp'=4] {'ep'}, use_global_device_ids=true, to_apply=%region_6.7 | all-reduce | flops 1 | bytes 8 | tf_op jit(solution)/shard_map/psum | solution.py:31
  115.6 18.4 %reduce-scatter.5.cloned.1.call-done = bf16[32,1792]{1,0:T(8,128)(2,1)} async-done(((bf16[32,7168]{1,0:T(8,128)(2,1)}), bf16[32,1792]{1,0:T(8,128)(2,1)}) %reduce-scatter.5.cloned.1.call-update) | async-done | bytes 114704 | tf_op jit(solution)/shard_map/reduce_scatter | solution.py:29
  (8 shorter events, 0.0 us)
Async XLA Ops:
  7.2 26.2 %all-gather.3.cloned.1.call-start = ((), (), s32[]{:S(2)}) async-start(), calls=%async_computation.2 | async-start | bytes 2293760 | tf_op jit(solution)/shard_map/all_gather | solution.py:20
  7.9 101.9 %reduce-scatter.3.cloned.1.call-start = ((), (), s32[]{:S(2)}) async-start(), calls=%async_computation.3 | async-start | bytes 2293760 | tf_op jit(solution)/shard_map/reduce_scatter | solution.py:28
  33.4 17.8 %copy-start.2 = (bf16[128,7168]{1,0:T(8,128)(2,1)S(1)}, bf16[128,7168]{1,0:T(8,128)(2,1)}, u32[]{:S(2)}) copy-start(bf16[128,7168]{1,0:T(8,128)(2,1)} %all-gather.3.cloned.1.call-done) | copy-start | bytes 5505028
  51.2 58.6 %copy-start = (s32[4,8]{1,0:T(4,128)S(1)}, s32[4,8]{1,0:T(4,128)}, u32[]{:S(2)}) copy-start(s32[4,8]{1,0:T(4,128)} %param.15) | copy-start | bytes 388
  51.2 58.6 %copy-start.1 = (s32[4]{0:T(128)S(1)}, s32[4]{0:T(128)}, u32[]{:S(2)}) copy-start(s32[4]{0:T(128)} %param.14) | copy-start | bytes 52
  80.0 54.0 %reduce-scatter.5.cloned.1.call-start = ((), (), s32[]{:S(2)}) async-start(), calls=%async_computation.4 | async-start | bytes 573440 | tf_op jit(solution)/shard_map/reduce_scatter | solution.py:29
Sparse Core Ops, SparseCore 0:
  9.5 23.8 all-gather.2
  80.2 29.5 reduce-scatter.2
  112.6 21.3 reduce-scatter.4
where the time goes:
time: 141 us
  waiting for transfers between devices  65 us (46%)
  matrix products  46.6 us (33%)
  between operations  13.8 us (10%)
  blocking collectives  11.1 us (8%)
  other arithmetic  3.75 us (3%)
    reduce_scatter x1, waiting for transfers between devices, per_device(): partial = lax.psum_scatter(partial, 'ep', scatter_dimension=0, tiled=True)  29.7 us
    reduce_scatter x1, waiting for transfers between devices, per_device(): mixed = lax.psum_scatter(partial, 'tp', scatter_dimension=1, tiled=True)  18.4 us
    dot_general x1, matrix products, per_device(): jnp.einsum('md,edf->emf', rows, w_gate, preferred_element_type=jnp.float32)  17.8 us
    all_gather x1, waiting for transfers between devices, per_device(): rows = lax.all_gather(tokens, 'ep', axis=0, tiled=True)  16.2 us
    dot_general x1, matrix products, per_device(): jnp.einsum('emf,efd->md', hidden, w_down, preferred_element_type=jnp.floa...  14.8 us
    dot_general x1, matrix products, per_device(): jnp.einsum('md,edf->emf', rows, w_up, preferred_element_type=jnp.float32)  14 us
    all_gather x1, blocking collectives, per_device(): dense = lax.all_gather(dense, 'ep', axis=0, tiled=True)  6.21 us
    psum x1, blocking collectives, per_device(): accepted = lax.psum(jnp.sum(jnp.cumprod(passed, axis=1)), 'ep').reshape(1)  4.89 us
  transfers between devices with their start and end apart: 3, of which 3 were waited for; matrix products, arithmetic and copies ran while one was open for 3% of the time, Pallas kernels for 0%

commit v1 on v0

--- a/solution.py
+++ b/solution.py
@@ -17,8 +17,11 @@
     named = expert_ids[:, :, None] == jnp.arange(EXPERTS, dtype=jnp.int32)[None, None, :]
     dense = jnp.sum(jnp.where(named, gates[:, :, None], 0.0), axis=1)
     dense = jnp.where(live.reshape(tok_rows)[:, None], dense, 0.0)
-    rows = lax.all_gather(tokens, "ep", axis=0, tiled=True)
-    dense = lax.all_gather(dense, "ep", axis=0, tiled=True)
+    rows, dense = jnp.split(
+        lax.all_gather(jnp.concatenate([tokens, dense], axis=1), "ep", axis=0, tiled=True),
+        [tokens.shape[1]],
+        axis=1,
+    )
     mine = lax.dynamic_slice_in_dim(dense, me * local, local, axis=1)
     gate = jnp.einsum("md,edf->emf", rows, w_gate, preferred_element_type=jnp.float32)
     up = jnp.einsum("md,edf->emf", rows, w_up, preferred_element_type=jnp.float32)

time: 141 us -> 151 us (1.071)
  waiting for transfers between devices: 65 us -> 82.8 us
  blocking collectives: 11.1 us -> 4.89 us
  matrix products: 46.6 us -> 41.5 us
  other arithmetic: 3.75 us -> 5.88 us
    all_gather x1, waiting for transfers between devices: 16.2 us -> 34.7 us  [per_device(): lax.all_gather(jnp.concatenate([tokens, dense], axis=1), 'ep', axis=0, ti...]
    all_gather x1 -> x0, blocking collectives: 6.21 us -> none  [per_device(): dense = lax.all_gather(dense, 'ep', axis=0, tiled=True)]
    dot_general x1, matrix products: 17.8 us -> 12.7 us  [per_device(): jnp.einsum('md,edf->emf', rows, w_gate, preferred_element_type=jnp.float32)]
  transfers between devices with their start and end apart: 3 -> 3, of which waited for: 3 -> 3; matrix products, arithmetic and copies ran while one was open for 3% -> 1% of each run, Pallas kernels for 0% -> 0%
where the time goes in v1:
time: 151 us; the launch traced here: 150 us
  waiting for transfers between devices  82.8 us (55%)
  matrix products  41.5 us (27%)
  between operations  13.8 us (9%)
  other arithmetic  5.88 us (4%)
  blocking collectives  4.89 us (3%)
    all_gather x1, waiting for transfers between devices, per_device(): lax.all_gather(jnp.concatenate([tokens, dense], axis=1), 'ep', axis=0, ti...  34.7 us
    reduce_scatter x1, waiting for transfers between devices, per_device(): partial = lax.psum_scatter(partial, 'ep', scatter_dimension=0, tiled=True)  29.7 us
    reduce_scatter x1, waiting for transfers between devices, per_device(): mixed = lax.psum_scatter(partial, 'tp', scatter_dimension=1, tiled=True)  18.4 us
    dot_general x1, matrix products, per_device(): jnp.einsum('emf,efd->md', hidden, w_down, preferred_element_type=jnp.floa...  15.2 us
    dot_general x1, matrix products, per_device(): jnp.einsum('md,edf->emf', rows, w_up, preferred_element_type=jnp.float32)  13.7 us
    dot_general x1, matrix products, per_device(): jnp.einsum('md,edf->emf', rows, w_gate, preferred_element_type=jnp.float32)  12.7 us
    psum x1, blocking collectives, per_device(): accepted = lax.psum(jnp.sum(jnp.cumprod(passed, axis=1)), 'ep').reshape(1)  4.89 us
  transfers between devices with their start and end apart: 3, of which 3 were waited for; matrix products, arithmetic and copies ran while one was open for 1% of the time, Pallas kernels for 0%

profile of v1, /device:TPU:0, one launch (start us, length us, event | category | flops | bytes accessed | tf_op | source)
XLA Modules:
  0.0 150.2 jit_solution(10053839081609812474)
XLA Ops:
  7.2 1.1 convert_element_type.10
  8.3 0.7 fusion.8
  9.0 0.7 multiply_divide_fusion
  9.7 0.7 select_reduce_fusion
  10.4 0.1 copy.13
  10.5 0.7 iota_compare_fusion.1
  11.2 0.1 lt.26
  11.3 0.1 broadcast_select_fusion
  11.4 1.0 pad_maximum_fusion
  12.4 0.0 reduce-scatter.3.cloned.1.call-start
  12.4 34.7 %all-gather.2.cloned.1.call-done = f32[128,7184]{1,0:T(8,128)} async-done(((f32[32,7184]{1,0:T(8,128)}), f32[128,7184]{1,0:T(8,128)}) %all-gather.2.cloned.1.call-update) | async-done | bytes 3678224 | tf_op jit(solution)/shard_map/all_gather | solution.py:21
  47.1 0.8 split.9
  48.0 0.1 dynamic-slice_bitcast_fusion
  48.0 0.1 copy.14
  48.1 12.7 %fusion.3 = f32[4,128,512]{2,1,0:T(8,128)S(1)} fusion(bf16[4,7168,512]{2,1,0:T(8,128)(2,1)} %param.9, f32[128,7184]{1,0:T(8,128)} %all-gather.2.cloned.1.call-done), kind=kOutput, calls=%fused_computation.5 | convolution fusion | flops 3758096384 | bytes 32243712 | tf_op jit(solution)/shard_map/md,edf->emf/dot_general | solution.py:26
  60.8 13.7 %fusion.7 = bf16[4,128,512]{2,1,0:T(8,128)(2,1)S(1)} fusion(bf16[4,7168,512]{2,1,0:T(8,128)(2,1)} %param.10, f32[128,7184]{1,0:T(8,128)S(1)} %copy-done, f32[4,128,512]{2,1,0:T(8,128)S(1)} %fusion.3, f32[4,128]{1,0:T(4,128)S(1)} %copy.14), kind=kOutput, calls=%fused_computation.9 | convolution fusion | flops 3759931392 | bytes 32770048 | tf_op jit(solution)/shard_map/md,edf->emf/dot_general | solution.py:27
  74.5 15.2 %fusion = bf16[128,7168]{1,0:T(8,128)(2,1)} fusion(bf16[4,128,512]{2,1,0:T(8,128)(2,1)S(1)} %fusion.7, bf16[4,512,7168]{2,1,0:T(8,128)(2,1)} %param.11), kind=kOutput, calls=%fused_computation.1 | convolution fusion | flops 3759013888 | bytes 31719424 | tf_op jit(solution)/shard_map/emf,efd->md/dot_general | solution.py:29
  89.7 0.0 reduce-scatter.5.cloned.1.call-start
  89.7 29.7 %reduce-scatter.3.cloned.1.call-done = bf16[32,7168]{1,0:T(8,128)(2,1)} async-done(((bf16[128,7168]{1,0:T(8,128)(2,1)}), bf16[32,7168]{1,0:T(8,128)(2,1)}) %reduce-scatter.3.cloned.1.call-update) | async-done | bytes 458768 | tf_op jit(solution)/shard_map/reduce_scatter | solution.py:31
  119.5 0.1 broadcast_select_fusion.1
  119.6 0.2 reduce_window.9
  119.7 0.6 reduce_sum.29
  120.4 4.9 %psum.7 = s32[1]{0:T(128)} all-reduce(s32[1]{0:T(128)} %bitcast.5), channel_id=1, replica_groups=mesh['groups'=2,'ep'=4,'tp'=4] {'ep'}, use_global_device_ids=true, to_apply=%region_6.7 | all-reduce | flops 1 | bytes 8 | tf_op jit(solution)/shard_map/psum | solution.py:34
  125.3 18.4 %reduce-scatter.5.cloned.1.call-done = bf16[32,1792]{1,0:T(8,128)(2,1)} async-done(((bf16[32,7168]{1,0:T(8,128)(2,1)}), bf16[32,1792]{1,0:T(8,128)(2,1)}) %reduce-scatter.5.cloned.1.call-update) | async-done | bytes 114704 | tf_op jit(solution)/shard_map/reduce_scatter | solution.py:32
  (10 shorter events, 0.1 us)
Async XLA Ops:
  7.2 40.0 %all-gather.2.cloned.1.call-start = ((), (), s32[]{:S(2)}) async-start(), calls=%async_computation.2 | async-start | bytes 4669440 | tf_op jit(solution)/shard_map/all_gather | solution.py:21
  12.4 107.0 %reduce-scatter.3.cloned.1.call-start = ((), (), s32[]{:S(2)}) async-start(), calls=%async_computation.3 | async-start | bytes 2293760 | tf_op jit(solution)/shard_map/reduce_scatter | solution.py:31
  48.1 12.7 %copy-start = (f32[128,7184]{1,0:T(8,128)S(1)}, f32[128,7184]{1,0:T(8,128)}, u32[]{:S(2)}) copy-start(f32[128,7184]{1,0:T(8,128)} %all-gather.2.cloned.1.call-done) | copy-start | bytes 11034628
  74.5 45.0 %copy-start.1 = (s32[4,8]{1,0:T(4,128)S(1)}, s32[4,8]{1,0:T(4,128)}, u32[]{:S(2)}) copy-start(s32[4,8]{1,0:T(4,128)} %param.15) | copy-start | bytes 388
  74.5 45.0 %copy-start.2 = (s32[4]{0:T(128)S(1)}, s32[4]{0:T(128)}, u32[]{:S(2)}) copy-start(s32[4]{0:T(128)} %param.14) | copy-start | bytes 52
  89.7 54.0 %reduce-scatter.5.cloned.1.call-start = ((), (), s32[]{:S(2)}) async-start(), calls=%async_computation.4 | async-start | bytes 573440 | tf_op jit(solution)/shard_map/reduce_scatter | solution.py:32
Sparse Core Ops, SparseCore 0:
  12.5 34.5 all-gather.1
  89.8 29.5 reduce-scatter.2
  122.3 21.3 reduce-scatter.4

commit v2 on v0

--- a/solution.py
+++ b/solution.py
@@ -17,7 +17,12 @@
     named = expert_ids[:, :, None] == jnp.arange(EXPERTS, dtype=jnp.int32)[None, None, :]
     dense = jnp.sum(jnp.where(named, gates[:, :, None], 0.0), axis=1)
     dense = jnp.where(live.reshape(tok_rows)[:, None], dense, 0.0)
-    rows = lax.all_gather(tokens, "ep", axis=0, tiled=True)
+    ring = [tokens]
+    for hop in range(3):
+        ring.append(lax.ppermute(ring[-1], "ep", [(dev, (dev + 1) % 4) for dev in range(4)]))
+    rows = jnp.roll(
+        jnp.concatenate(ring[::-1], axis=0), (lax.axis_index("ep") + 1) * ring[0].shape[0], axis=0
+    )
     dense = lax.all_gather(dense, "ep", axis=0, tiled=True)
     mine = lax.dynamic_slice_in_dim(dense, me * local, local, axis=1)
     gate = jnp.einsum("md,edf->emf", rows, w_gate, preferred_element_type=jnp.float32)

time: 141 us -> 133 us (0.943)
  matrix products: 46.6 us -> 33.6 us
  local copies, waits for them, and re-layouts: 0.21 us -> 3.27 us
    all_gather x1 -> x0, waiting for transfers between devices: 16.2 us -> none  [per_device(): rows = lax.all_gather(tokens, 'ep', axis=0, tiled=True)]
    ppermute x0 -> x3, waiting for transfers between devices: none -> 14.7 us  [per_device(): lax.ppermute(ring[-1], 'ep', [(dev, (dev + 1) % 4) for dev in range(4)])]
    dot_general x1 -> x0, matrix products: 14 us -> none  [per_device(): jnp.einsum('md,edf->emf', rows, w_up, preferred_element_type=jnp.float32)]
    dot_general x1, matrix products: 14.8 us -> 22.2 us  [per_device(): jnp.einsum('emf,efd->md', hidden, w_down, preferred_element_type=jnp.floa...]
    dot_general x1, matrix products: 17.8 us -> 11.4 us  [per_device(): jnp.einsum('md,edf->emf', rows, w_gate, preferred_element_type=jnp.float32)]
    unnamed x7 -> x16, local copies, waits for them, and re-layouts: 0.1 us -> 3.13 us
    reduce_scatter x1, waiting for transfers between devices: 29.7 us -> 31.7 us  [per_device(): partial = lax.psum_scatter(partial, 'ep', scatter_dimension=0, tiled=True)]
  transfers between devices with their start and end apart: 3 -> 5, of which waited for: 3 -> 4; matrix products, arithmetic and copies ran while one was open for 3% -> 3% of each run, Pallas kernels for 0% -> 0%
where the time goes in v2:
time: 133 us
  waiting for transfers between devices  64.9 us (49%)
  matrix products  33.6 us (25%)
  between operations  14.2 us (11%)
  blocking collectives  12.2 us (9%)
  other arithmetic  3.74 us (3%)
  local copies, waits for them, and re-layouts  3.27 us (2%)
    reduce_scatter x1, waiting for transfers between devices, per_device(): partial = lax.psum_scatter(partial, 'ep', scatter_dimension=0, tiled=True)  31.7 us
    dot_general x1, matrix products, per_device(): jnp.einsum('emf,efd->md', hidden, w_down, preferred_element_type=jnp.floa...  22.2 us
    reduce_scatter x1, waiting for transfers between devices, per_device(): mixed = lax.psum_scatter(partial, 'tp', scatter_dimension=1, tiled=True)  18.4 us
    ppermute x3, waiting for transfers between devices, per_device(): lax.ppermute(ring[-1], 'ep', [(dev, (dev + 1) % 4) for dev in range(4)])  14.7 us
    dot_general x1, matrix products, per_device(): jnp.einsum('md,edf->emf', rows, w_gate, preferred_element_type=jnp.float32)  11.4 us
    all_gather x1, blocking collectives, per_device(): dense = lax.all_gather(dense, 'ep', axis=0, tiled=True)  7.28 us
    psum x1, blocking collectives, per_device(): accepted = lax.psum(jnp.sum(jnp.cumprod(passed, axis=1)), 'ep').reshape(1)  4.89 us
    unnamed x16, local copies, waits for them, and re-layouts  3.13 us
  transfers between devices with their start and end apart: 5, of which 4 were waited for; matrix products, arithmetic and copies ran while one was open for 3% of the time, Pallas kernels for 0%

profile of v2, /device:TPU:0, one launch (start us, length us, event | category | flops | bytes accessed | tf_op | source)
XLA Modules:
  0.0 132.5 jit_solution(2306946564197831017)
XLA Ops:
  7.2 0.0 reduce-scatter.3.cloned.1.call-start
  7.2 0.5 collective-permute-start
  7.8 8.3 %collective-permute-done = bf16[32,7168]{1,0:T(8,128)(2,1)S(1)} collective-permute-done((bf16[32,7168]{1,0:T(8,128)(2,1)}, bf16[32,7168]{1,0:T(8,128)(2,1)S(1)}, u32[]{:S(2)}, u32[]{:S(2)}) %collective-permute-start) | collective-permute-done | bytes 458784 | tf_op jit(solution)/shard_map/ppermute | solution.py:22
  16.1 0.0 collective-permute-start.1
  16.1 0.7 fusion.15
  16.8 0.7 multiply_divide_fusion
  17.5 6.5 %collective-permute-done.1 = bf16[32,7168]{1,0:T(8,128)(2,1)S(1)} collective-permute-done((bf16[32,7168]{1,0:T(8,128)(2,1)S(1)}, bf16[32,7168]{1,0:T(8,128)(2,1)S(1)}, u32[]{:S(2)}, u32[]{:S(2)}) %collective-permute-start.1) | collective-permute-done | bytes 458784 | tf_op jit(solution)/shard_map/ppermute | solution.py:22
  24.0 0.7 iota_compare_fusion.1
  24.7 0.1 lt.40
  24.8 0.7 select_reduce_fusion
  25.5 7.3 %all-gather = f32[4,32,16]{1,2,0:T(8,128)S(1)} all-gather(f32[1,32,16]{1,2,0:T(8,128)S(1)} %select_bitcast_fusion), channel_id=1, replica_groups=mesh['groups'=2,'ep'=4,'tp'=4] {'ep'}, dimensions={0}, use_global_device_ids=true | all-gather | bytes 10240 | tf_op jit(solution)/shard_map/all_gather | solution.py:26
  32.8 0.1 reshape.28
  33.0 1.1 constant_dynamic-update-slice_fusion.4
  34.2 1.8 %copy-done.1 = bf16[256,7168]{1,0:T(8,128)(2,1)} copy-done((bf16[256,7168]{1,0:T(8,128)(2,1)}, bf16[256,7168]{1,0:T(8,128)(2,1)S(1)}, u32[]{:S(2)}) %copy-start.1) | copy-done | bytes 3670040
  36.0 11.4 %fusion.7 = f32[4,128,512]{2,1,0:T(8,128)S(1)} fusion(bf16[4,7168,512]{2,1,0:T(8,128)(2,1)} %param.9, bf16[256,7168]{1,0:T(8,128)(2,1)S(1)} %constant_dynamic-update-slice_fusion, s32[]{:T(128)S(6)} %select_n.25), kind=kOutput, calls=%fused_computation.8 | convolution fusion | flops 3758096384 | bytes 32243716 | tf_op jit(solution)/shard_map/md,edf->emf/dot_general | solution.py:28
  47.5 22.2 %fusion = bf16[128,7168]{1,0:T(8,128)(2,1)} fusion(bf16[4,512,7168]{2,1,0:T(8,128)(2,1)} %param.11, f32[4,128,512]{2,1,0:T(8,128)S(1)} %fusion.7, f32[4,128]{1,0:T(4,128)S(1)} %dynamic-slice_bitcast_fusion, bf16[4,7168,512]{2,1,0:T(8,128)(2,1)} %param.10, bf16[256,7168]{1,0:T(8,128)(2,1)} %copy-done.1, s32[]{:T(128)S(6)} %select_n.25), kind=kOutput, calls=%fused_computation.1 | convolution fusion | flops 7518945280 | bytes 63440900 | tf_op jit(solution)/shard_map/emf,efd->md/dot_general | solution.py:31
  69.7 0.0 reduce-scatter.3.cloned.1.call-update
  69.7 0.0 reduce-scatter.5.cloned.1.call-start
  69.7 31.7 %reduce-scatter.3.cloned.1.call-done = bf16[32,7168]{1,0:T(8,128)(2,1)} async-done(((bf16[128,7168]{1,0:T(8,128)(2,1)}), bf16[32,7168]{1,0:T(8,128)(2,1)}) %reduce-scatter.3.cloned.1.call-update) | async-done | bytes 458768 | tf_op jit(solution)/shard_map/reduce_scatter | solution.py:33
  101.5 0.1 broadcast_select_fusion
  101.6 0.2 reduce_window.9
  101.8 0.6 reduce_sum.29
  102.4 4.9 %psum.7 = s32[1]{0:T(128)} all-reduce(s32[1]{0:T(128)} %bitcast.6), channel_id=1, replica_groups=mesh['groups'=2,'ep'=4,'tp'=4] {'ep'}, use_global_device_ids=true, to_apply=%region_6.7 | all-reduce | flops 1 | bytes 8 | tf_op jit(solution)/shard_map/psum | solution.py:36
  107.3 18.4 %reduce-scatter.5.cloned.1.call-done = bf16[32,1792]{1,0:T(8,128)(2,1)} async-done(((bf16[32,7168]{1,0:T(8,128)(2,1)}), bf16[32,1792]{1,0:T(8,128)(2,1)}) %reduce-scatter.5.cloned.1.call-update) | async-done | bytes 114704 | tf_op jit(solution)/shard_map/reduce_scatter | solution.py:34
  (20 shorter events, 0.3 us)
Async XLA Ops:
  7.2 27.0 %copy-start = (bf16[32,7168]{1,0:T(8,128)(2,1)S(1)}, bf16[32,7168]{1,0:T(8,128)(2,1)}, u32[]{:S(2)}) copy-start(bf16[32,7168]{1,0:T(8,128)(2,1)} %param.8) | copy-start | bytes 1376260
  7.2 94.3 %reduce-scatter.3.cloned.1.call-start = ((), (), s32[]{:S(2)}) async-start(), calls=%async_computation.2 | async-start | bytes 2293760 | tf_op jit(solution)/shard_map/reduce_scatter | solution.py:33
  7.2 8.8 %collective-permute-start = (bf16[32,7168]{1,0:T(8,128)(2,1)}, bf16[32,7168]{1,0:T(8,128)(2,1)S(1)}, u32[]{:S(2)}, u32[]{:S(2)}) collective-permute-start(bf16[32,7168]{1,0:T(8,128)(2,1)} %param.8), channel_id=1, source_target_pairs={{0,4},{4,8},{8,12},{12,0},{1,5},{5,9},{9,13},{13,1},{2,6},{6,10},{... | collective-permute-start | bytes 1376264 | tf_op jit(solution)/shard_map/ppermute | solution.py:22
  16.1 7.9 %collective-permute-start.1 = (bf16[32,7168]{1,0:T(8,128)(2,1)S(1)}, bf16[32,7168]{1,0:T(8,128)(2,1)S(1)}, u32[]{:S(2)}, u32[]{:S(2)}) collective-permute-start(bf16[32,7168]{1,0:T(8,128)(2,1)S(1)} %collective-permute-done), channel_id=1, source_target_pairs={{0,4},{4,8},{8,12},{12,0},{1,5},{5,9},{9,13},{13,1},{2,6},{6,10},{... | collective-permute-start | bytes 1376264 | tf_op jit(solution)/shard_map/ppermute | solution.py:22
  24.0 8.9 %collective-permute-start.2 = (bf16[32,7168]{1,0:T(8,128)(2,1)S(1)}, bf16[32,7168]{1,0:T(8,128)(2,1)S(1)}, u32[]{:S(2)}, u32[]{:S(2)}) collective-permute-start(bf16[32,7168]{1,0:T(8,128)(2,1)S(1)} %collective-permute-done.1), channel_id=1, source_target_pairs={{0,4},{4,8},{8,12},{12,0},{1,5},{5,9},{9,13},{13,1},{2,6},{6,10},{... | collective-permute-start | bytes 1376264 | tf_op jit(solution)/shard_map/ppermute | solution.py:22
  34.2 1.8 %copy-start.1 = (bf16[256,7168]{1,0:T(8,128)(2,1)}, bf16[256,7168]{1,0:T(8,128)(2,1)S(1)}, u32[]{:S(2)}) copy-start(bf16[256,7168]{1,0:T(8,128)(2,1)S(1)} %constant_dynamic-update-slice_fusion) | copy-start | bytes 11010052
  47.5 54.0 %copy-start.2 = (s32[4,8]{1,0:T(4,128)S(1)}, s32[4,8]{1,0:T(4,128)}, u32[]{:S(2)}) copy-start(s32[4,8]{1,0:T(4,128)} %param.15) | copy-start | bytes 388
  47.5 54.0 %copy-start.3 = (s32[4]{0:T(128)S(1)}, s32[4]{0:T(128)}, u32[]{:S(2)}) copy-start(s32[4]{0:T(128)} %param.14) | copy-start | bytes 52
  69.7 56.0 %reduce-scatter.5.cloned.1.call-start = ((), (), s32[]{:S(2)}) async-start(), calls=%async_computation.3 | async-start | bytes 573440 | tf_op jit(solution)/shard_map/reduce_scatter | solution.py:34
Sparse Core Ops, SparseCore 0:
  69.8 31.6 reduce-scatter.2
  104.3 21.2 reduce-scatter.4
